TPU v7x, 256 devices: a whole 4x4x8 slice. The times are simulated.
256 devices in a mesh: sa: 64 (over y_hi, z, x), ka: 2 (over y_lo), vert: 2 (over core).
Axes of the slice: x: 4, y: 4 (y_hi: 2, y_lo: 2; y = y_hi * 2 + y_lo), z: 8, core: 2. Of those that a mesh axis runs over, the one named last changes fastest.
Arguments:
- queries: bfloat16 [8192, 16, 128], P('sa', None, 'ka'), may hold values from -6 to 6
- key_rows: bfloat16 [8192, 16, 128], P('sa', None, 'ka'), may hold values from -6 to 6
- values: bfloat16 [8192, 16, 256], P('sa', None, 'vert'), may hold values from -6 to 6
- log_decays: bfloat16 [8192, 16, 128], P('sa', None, 'ka'), may hold values from -2 to 0
- output_grad: bfloat16 [8192, 16, 256], P('sa', None, 'vert'), may hold values from -0.0625 to 0.0625
Outputs:
- query_grad: float32 [8192, 16, 128], P('sa', 'vert', 'ka')
- key_grad: float32 [8192, 16, 128], P('sa', 'vert', 'ka')
- value_grad: float32 [8192, 16, 256], P('sa', 'ka', 'vert')
- decay_grad: float32 [8192, 16, 128], P('sa', 'vert', 'ka')
All inputs are finite; a program needn't handle non-finite values.
Results may differ from a plain program's by a relative error of at most 0.0003.
Values may be sent and summed in bfloat16 or wider, within the bound.
A program may use at most 192 MiB of HBM per device.

v0:
```python
import jax
import jax.numpy as jnp
from jax import lax
from jax.sharding import Mesh
from jax.sharding import PartitionSpec as P

DK = 128
TILE_LEN = 64
SA = ("sa_0", "sa_1", "sa_2")


largest_entry = lax.Precision.HIGHEST


def nothing_yet(shard, identity):
    return jax.tree.map(
        lambda a, e: jnp.broadcast_to(jnp.asarray(e, a.dtype), a.shape), shard, identity
    )


def prefix_by_axis(shard, axes, combine, identity, reverse):
    before = start = nothing_yet(shard, identity)
    total = shard
    for axis in reversed(axes):
        length, place = (lax.axis_size(axis), lax.axis_index(axis))
        pieces = jax.tree.map(lambda part: lax.all_gather(part, axis), total)
        inside, total = (start, start)
        for k in reversed(range(length)) if reverse else range(length):
            passed = k > place if reverse else k < place
            total = combine(total, jax.tree.map(lambda part: part[k], pieces))
            inside = jax.tree.map(lambda new, old: jnp.where(passed, new, old), total, inside)
        before = combine(inside, before)
    return before


def from_everyone(shard, axis):
    copies = jnp.broadcast_to(shard, (lax.axis_size(axis), *shard.shape))
    return lax.all_to_all(copies, axis, split_axis=0, concat_axis=0, tiled=True)


def folded_in_pairs(pieces, combine):
    while len(jax.tree.leaves(pieces)[0]) > 1:
        pieces = jax.vmap(combine)(*(pieces[side::2] for side in (0, 1)))
    return pieces[0]


def carried_in(shard, axis, combine, identity):
    length, place = (lax.axis_size(axis), lax.axis_index(axis))
    passed = jnp.arange(length) > place

    def kept(part, zero, own):
        part = jnp.where(
            passed.reshape(-1, *(1 for _ in own.shape)), part, jnp.asarray(zero, own.dtype)
        )
        return part[::-1]

    pieces = from_everyone(shard, axis)
    return folded_in_pairs(kept(pieces, identity, shard), combine)


def cut_along(shard, dim, length):
    dims = shard.shape
    parts = shard.reshape(*dims[:dim], length, dims[dim] // length, *dims[dim + 1 :])
    return jnp.moveaxis(parts, dim, 0)


def summed_on_arrival(shard, axis, dim):
    parts = cut_along(shard, dim, lax.axis_size(axis))
    arrived = lax.all_to_all(parts, axis, split_axis=0, concat_axis=0, tiled=True)
    return arrived.sum(axis=0)


def sent_together(arrays, axis, split_dim, concat_dim, along):
    widths = [a.shape[along] for a in arrays]
    both = jnp.concatenate(arrays, axis=along)
    filled = lax.all_to_all(both, axis, split_axis=split_dim, concat_axis=concat_dim, tiled=True)
    return tuple(jnp.split(filled, [sum(widths[:k]) for k in range(1, len(widths))], axis=along))


def to_blocks(tensor, length):
    row_count, head_count, channels = tensor.shape
    return (
        tensor.astype(jnp.float32)
        .reshape(row_count // length, length, head_count, channels)
        .transpose(0, 2, 1, 3)
    )


def from_blocks(tensor):
    tile_count, head_count, length, channels = tensor.shape
    return tensor.transpose(0, 2, 1, 3).reshape(tile_count * length, head_count, channels)


def causal(length):
    row_ids = lax.broadcasted_iota(jnp.int32, (length, length), 0)
    col_ids = lax.broadcasted_iota(jnp.int32, (length, length), 1)
    return row_ids >= col_ids


def compose(earlier, later):
    return (earlier[0] * later[0], later[0][..., None] * earlier[1] + later[1])


def add_terms(earlier, later):
    return earlier + later


def advance(carried_over, step_terms):
    return (step_terms[0][..., None] * carried_over + step_terms[1], carried_over)


def backward_states(scaled, cumulative, cotangent):
    tile_total = cumulative[:, :, -1, :]
    amplified_query = scaled * jnp.exp(cumulative)
    terms = jnp.einsum("nhik,nhiv->nhkv", amplified_query, cotangent, precision=largest_entry)
    leading, ends = lax.scan(
        advance, jnp.zeros_like(terms[0]), (jnp.exp(tile_total), terms), reverse=True
    )
    after = jnp.sum(tile_total, 0) - jnp.cumsum(tile_total, 0)
    return (amplified_query, ends, leading, after)


def value_terms(amplified_query, shrunk_key, attenuated_key, cotangent, ends, lower_mask):
    weights = jnp.where(
        lower_mask,
        jnp.einsum("nhik,nhjk->nhij", amplified_query, shrunk_key, precision=largest_entry),
        0.0,
    )
    local_part = jnp.einsum("nhij,nhiv->nhjv", weights, cotangent, precision=largest_entry)
    return local_part + jnp.einsum("nhjk,nhkv->nhjv", attenuated_key, ends, precision=largest_entry)


def gradient_core(queries, key_rows, values, log_decays, output_grad):
    factor = DK ** (-0.5)
    scaled = to_blocks(queries, TILE_LEN) * factor
    keyed = to_blocks(key_rows, TILE_LEN)
    valued = to_blocks(values, TILE_LEN)
    cotangent = to_blocks(output_grad, TILE_LEN)
    cumulative = jnp.cumsum(to_blocks(log_decays, TILE_LEN), axis=2)
    tile_total = cumulative[:, :, -1, :]
    growth = jnp.exp(cumulative)
    shrink = jnp.exp(-cumulative)
    until_finish = jnp.exp(tile_total[:, :, None, :] - cumulative)
    shrunk_key = keyed * shrink
    attenuated_key = keyed * until_finish
    forward_terms = jnp.einsum("nhjk,nhjv->nhkv", attenuated_key, valued, precision=largest_entry)
    shard_state, starts = lax.scan(
        advance, jnp.zeros_like(forward_terms[0]), (jnp.exp(tile_total), forward_terms)
    )
    amplified_query, ends, shard_back, after = backward_states(scaled, cumulative, cotangent)
    shard_decay = jnp.exp(jnp.sum(tile_total, 0))
    identity = (jnp.ones_like(shard_decay), jnp.zeros_like(shard_state))
    incoming = prefix_by_axis((shard_decay, shard_state), SA, compose, identity, False)[1]
    outgoing = prefix_by_axis((shard_decay, shard_back), SA, compose, identity, True)[1]
    before = jnp.cumsum(tile_total, 0) - tile_total
    starts = starts + jnp.exp(before)[..., None] * incoming[None]
    ends = ends + jnp.exp(after)[..., None] * outgoing[None]
    lower_mask = causal(TILE_LEN)
    scores = jnp.where(
        lower_mask, jnp.einsum("nhiv,nhjv->nhij", cotangent, valued, precision=largest_entry), 0.0
    )
    query_local = jnp.einsum("nhij,nhjk->nhik", scores, shrunk_key, precision=largest_entry)
    query_carried = jnp.einsum("nhiv,nhkv->nhik", cotangent, starts, precision=largest_entry)
    query_part = growth * (query_local + query_carried) * factor
    key_local = shrink * jnp.einsum(
        "nhij,nhik->nhjk", scores, amplified_query, precision=largest_entry
    )
    key_part = key_local + until_finish * jnp.einsum(
        "nhjv,nhkv->nhjk", valued, ends, precision=largest_entry
    )
    pieces = (amplified_query, shrunk_key, attenuated_key, cotangent, ends, lower_mask)
    return (query_part, key_part, pieces, outgoing)


def later_sums(position_grad):
    shard_rows = position_grad.shape[0]
    head_span = position_grad.shape[1]
    tile_rows = position_grad.reshape(
        shard_rows // TILE_LEN, TILE_LEN, head_span, position_grad.shape[2]
    )
    upper = causal(TILE_LEN).T.astype(jnp.float32)
    within = jnp.einsum("ij,njhk->nihk", upper, tile_rows, precision=largest_entry)
    tile_sums = jnp.sum(tile_rows, 1)
    later = jnp.sum(tile_sums, 0) - jnp.cumsum(tile_sums, 0)
    shard_sum = jnp.sum(tile_sums, 0)
    beyond = carried_in(shard_sum, SA, add_terms, jnp.zeros_like(shard_sum))
    return (within + later[:, None] + beyond[None, None]).reshape(position_grad.shape)


def shards(queries, key_rows, values, log_decays, output_grad):
    factor = DK ** (-0.5)
    query_part, key_part, pieces, outgoing = gradient_core(
        queries, key_rows, values, log_decays, output_grad
    )
    amplified_query, shrunk_key, attenuated_key, cotangent, ends, lower_mask = pieces
    query_grad, key_grad = (
        summed_on_arrival(from_blocks(query_part), "vert", 1),
        summed_on_arrival(from_blocks(key_part), "vert", 1),
    )
    moved = sent_together((queries, key_rows, log_decays), "ka", 1, 2, 0)
    state_rows = lax.all_to_all(outgoing, "ka", split_axis=0, concat_axis=1, tiled=True)
    head_share = queries.shape[1] // lax.axis_size("ka")
    grad_rows = lax.dynamic_slice_in_dim(
        output_grad, lax.axis_index("ka") * head_share, head_share, 1
    )
    moved_cum = jnp.cumsum(to_blocks(moved[2], TILE_LEN), axis=2)
    moved_key = to_blocks(moved[1], TILE_LEN)
    moved_grad = to_blocks(grad_rows, TILE_LEN)
    moved_query, moved_ends, unused_start, moved_after = backward_states(
        to_blocks(moved[0], TILE_LEN) * factor, moved_cum, moved_grad
    )
    moved_ends = moved_ends + jnp.exp(moved_after)[..., None] * state_rows[None]
    moved_total = moved_cum[:, :, -1, :]
    moved_shrunk = moved_key * jnp.exp(-moved_cum)
    moved_faded = moved_key * jnp.exp(moved_total[:, :, None, :] - moved_cum)
    value_part = value_terms(
        moved_query, moved_shrunk, moved_faded, moved_grad, moved_ends, lower_mask
    )
    value_grad = from_blocks(value_part)
    head_half = queries.shape[1] // lax.axis_size("vert")
    first_head = lax.axis_index("vert") * head_half
    own_query = lax.dynamic_slice_in_dim(queries, first_head, head_half, 1).astype(jnp.float32)
    own_key = lax.dynamic_slice_in_dim(key_rows, first_head, head_half, 1).astype(jnp.float32)
    position_grad = own_query * query_grad - own_key * key_grad
    decay_grad = later_sums(position_grad)
    return (query_grad, key_grad, value_grad, decay_grad)


def solution(mesh):
    finer = Mesh(
        mesh.devices.reshape(2, 8, 4, mesh.shape["ka"], mesh.shape["vert"]),
        ("sa_0", "sa_1", "sa_2", "ka", "vert"),
    )
    in_specs = (
        P(SA, None, "ka"),
        P(SA, None, "ka"),
        P(SA, None, "vert"),
        P(SA, None, "ka"),
        P(SA, None, "vert"),
    )
    out_specs = (P(SA, "vert", "ka"), P(SA, "vert", "ka"), P(SA, "ka", "vert"), P(SA, "vert", "ka"))
    return jax.shard_map(
        shards, mesh=finer, in_specs=in_specs, out_specs=out_specs, check_vma=False
    )
```

profile of v0, /device:TPU:1, one launch (start us, length us, event | category | flops | bytes accessed | tf_op | source)
XLA Modules:
  0.0 340.2 jit_solution(493911150432388434)
XLA Ops:
  7.2 1.4 copy.134
  8.6 13.2 %fusion.93 = f32[2,16,64,64]{3,1,2,0:T(8,128)S(1)} fusion(f32[2,16,64,64]{3,1,2,0:T(8,128)S(1)} %bitcast.396), kind=kOutput, calls=%fused_computation.213 | output fusion | flops 8257536 | bytes 1048576 | tf_op jit(solution)/shard_map/jit(cumsum)/reduce_window_sum | solution.py:139
  23.3 1.6 mul.855
  25.0 1.3 copy.110
  26.3 2.5 fusion.19
  28.8 1.1 broadcast.298.clone.1
  29.9 2.3 while.48
  33.7 1.3 copy.104
  35.0 2.6 fusion.10
  37.6 1.1 broadcast.298.clone
  38.7 2.3 while.47
  41.9 10.2 %all-gather = f32[64,64]{1,0:T(8,128)S(1)} all-gather(f32[16,64]{1,0:T(8,128)S(1)} %exp.76), channel_id=2, replica_groups=mesh['sa_0'=2,'sa_1'=8,'sa_2'=4,'ka'=2,'vert'=2] {'sa_2'}, dimensions={0}, use_global_device_ids=true | all-gather | bytes 20480 | tf_op jit(solution)/shard_map/all_gather | solution.py:26
  52.1 18.0 %all-gather.20.cloned.1.call-done = f32[64,64,128]{2,1,0:T(8,128)} async-done(((f32[16,64,128]{2,1,0:T(8,128)}), f32[64,64,128]{2,1,0:T(8,128)}) %all-gather.20.cloned.1.call-update) | async-done | bytes 2097168 | tf_op jit(solution)/shard_map/all_gather | solution.py:26
  70.1 35.3 %all-gather.18.cloned.1.call-done = f32[64,64,128]{2,1,0:T(8,128)} async-done(((f32[16,64,128]{2,1,0:T(8,128)}), f32[64,64,128]{2,1,0:T(8,128)}) %all-gather.18.cloned.1.call-update) | async-done | bytes 2097168 | tf_op jit(solution)/shard_map/all_gather | solution.py:26
  105.4 3.5 %bitcast_add_fusion.13 = (f32[1,16,64,128]{3,2,1,0:T(8,128)}, f32[1,16,64,128]{3,2,1,0:T(8,128)}) fusion(f32[64,64,128]{2,1,0:T(8,128)} %all-gather.20.cloned.1.call-done, f32[16,64]{1,0:T(8,128)S(1)} %get-tuple-element.373, f32[16,64]{1,0:T(8,128)S(1)} %get-tuple-element.372, f32[16,64]{1,0:T(8,128)S(1)} %get-tuple-element.369, ...), kind=kLoop, calls=%fused_computation.90 | loop fusion | flops 1835008 | bytes 5267456 | tf_op jit(solution)/shard_map/add | solution.py:101
  109.5 1.0 pad_maximum_fusion
  110.5 4.3 %all-to-all-start.2 = ((bf16[384,16,64]{0,2,1:T(8,128)(2,1)}), bf16[384,16,64]{0,2,1:T(8,128)(2,1)}, u32[]{:S(2)}, u32[]{:S(2)}) async-start(bf16[384,16,64]{0,2,1:T(8,128)(2,1)} %pad_maximum_fusion), calls=%async_computation.2 | async-start | bytes 1572864 | tf_op jit(solution)/shard_map/all_to_all | solution.py:76
  115.0 22.1 %all_gather.51 = f32[8,16,64]{2,1,0:T(8,128)S(1)} all-gather(f32[1,16,64]{2,1,0:T(8,128)S(1)} %get-tuple-element.368), channel_id=1, replica_groups=mesh['sa_0'=2,'sa_1'=8,'sa_2'=4,'ka'=2,'vert'=2] {'sa_1'}, dimensions={0}, use_global_device_ids=true | all-gather | bytes 36864 | tf_op jit(solution)/shard_map/all_gather | solution.py:26
  137.7 4.7 %all_gather.52 = f32[2,16,64]{2,1,0:T(8,128)S(1)} all-gather(f32[1,16,64]{2,1,0:T(8,128)S(1)} %get-tuple-element.359), channel_id=1, replica_groups=mesh['sa_0'=2,'sa_1'=8,'sa_2'=4,'ka'=2,'vert'=2] {'sa_0'}, dimensions={0}, use_global_device_ids=true | all-gather | bytes 12288 | tf_op jit(solution)/shard_map/all_gather | solution.py:26
  142.4 21.7 %all_gather.57 = f32[8,16,64]{2,1,0:T(8,128)S(1)} all-gather(f32[1,16,64]{2,1,0:T(8,128)S(1)} %get-tuple-element.367), channel_id=1, replica_groups=mesh['sa_0'=2,'sa_1'=8,'sa_2'=4,'ka'=2,'vert'=2] {'sa_1'}, dimensions={0}, use_global_device_ids=true | all-gather | bytes 36864 | tf_op jit(solution)/shard_map/all_gather | solution.py:26
  164.7 5.0 %all_gather.58 = f32[2,16,64]{2,1,0:T(8,128)S(1)} all-gather(f32[1,16,64]{2,1,0:T(8,128)S(1)} %get-tuple-element.351), channel_id=1, replica_groups=mesh['sa_0'=2,'sa_1'=8,'sa_2'=4,'ka'=2,'vert'=2] {'sa_0'}, dimensions={0}, use_global_device_ids=true | all-gather | bytes 12288 | tf_op jit(solution)/shard_map/all_gather | solution.py:26
  173.4 1.4 convolution_select_fusion
  174.8 3.6 %copy.115 = bf16[384,2,8,64]{3,1,2,0:T(2,128)(2,1)S(1)} copy(bf16[384,2,8,64]{0,3,2,1:T(8,128)(2,1)} %bitcast.51) | data formatting | bytes 1572864 | tf_op jit(solution)/shard_map/all_to_all | solution.py:76
  178.5 2.1 slice_convert_fusion.1
  180.6 2.6 reshape.327
  183.2 2.6 reshape.326
  185.8 1.5 convert_multiply_fusion
  187.4 1.9 mul.920
  189.3 1.1 fusion.34
  191.0 1.0 bitcast_multiply_fusion.7
  192.1 1.0 convolution_select_fusion.1
  193.1 1.4 fusion.62
  194.5 1.0 fusion.52
  195.6 3.6 %slice_add_fusion.2 = (f32[1,16,64,128]{3,2,1,0:T(8,128)}, f32[1,16,64,128]{3,2,1,0:T(8,128)}) fusion(f32[8,16,64,128]{3,2,1,0:T(8,128)} %all-gather.10.cloned.1.call-done, f32[16,64]{1,0:T(8,128)S(1)} %get-tuple-element.361, f32[16,64]{1,0:T(8,128)S(1)} %copy-done.40, f32[16,64]{1,0:T(8,128)S(1)} %get-tuple-element.363, ...), kind=kLoop, calls=%fused_computation.53 | loop fusion | flops 1966080 | bytes 5275648 | tf_op jit(solution)/shard_map/add | solution.py:101
  199.5 1.1 broadcast_in_dim.87
  200.6 2.3 while.49
  202.9 17.5 %all-gather.14.cloned.1.call-done = f32[8,16,64,128]{3,2,1,0:T(8,128)} async-done(((f32[1,16,64,128]{3,2,1,0:T(8,128)}), f32[8,16,64,128]{3,2,1,0:T(8,128)}) %all-gather.14.cloned.1.call-update) | async-done | bytes 4194320 | tf_op jit(solution)/shard_map/all_gather | solution.py:26
  220.5 3.8 %multiply_add_fusion = (f32[1,16,64,128]{3,2,1,0:T(8,128)}, f32[1,16,64,128]{3,2,1,0:T(8,128)}) fusion(f32[8,16,64,128]{3,2,1,0:T(8,128)} %all-gather.14.cloned.1.call-done, f32[16,64]{1,0:T(8,128)S(1)} %get-tuple-element.353, f32[16,64]{1,0:T(8,128)S(1)} %copy-done.30, f32[16,64]{1,0:T(8,128)S(1)} %get-tuple-element.355, ...), kind=kLoop, calls=%fused_computation.107 | loop fusion | flops 1966080 | bytes 5275648 | tf_op jit(solution)/shard_map/add | solution.py:101
  224.3 24.3 %all-gather.12.cloned.1.call-done = f32[2,16,64,128]{3,2,1,0:T(8,128)} async-done(((f32[1,16,64,128]{3,2,1,0:T(8,128)}), f32[2,16,64,128]{3,2,1,0:T(8,128)}) %all-gather.12.cloned.1.call-update) | async-done | bytes 1048592 | tf_op jit(solution)/shard_map/all_gather | solution.py:26
  248.7 4.5 %fusion.23 = f32[16,64,128]{2,1,0:T(8,128)S(1)} fusion(f32[2,16,64,128]{3,2,1,0:T(8,128)} %all-gather.12.cloned.1.call-done, f32[1,16,64,128]{3,2,1,0:T(8,128)} %get-tuple-element.379, f32[1,16,64,128]{3,2,1,0:T(8,128)} %get-tuple-element.336, f32[1,16,64,128]{3,2,1,0:T(8,128)} %get-tuple-element.337, f32[8,16,64,128]{3,2,1,0:T(8,128)} %all-gather.10.cloned.1.call-done, ...), kind=kLoop, calls=%fused_computation.51 | loop fusion | flops 4849664 | bytes 7917582 | tf_op jit(solution)/shard_map/mul | solution.py:156
  253.2 1.1 convolution_bitcast_fusion.2
  254.7 3.0 fusion.4
  257.7 2.4 copy.109
  260.1 2.7 reshape_reshape.6
  262.8 5.0 %all-to-all-start = ((f32[2,128,8,64]{1,3,2,0:T(8,128)}), f32[2,128,8,64]{1,3,2,0:T(8,128)}, u32[]{:S(2)}, u32[]{:S(2)}) async-start(f32[2,128,8,64]{1,3,2,0:T(8,128)} %bitcast.399), calls=%async_computation | async-start | bytes 1048576 | tf_op jit(solution)/shard_map/all_to_all | solution.py:69
  267.9 9.7 %all-gather.16.cloned.1.call-done = f32[2,16,64,128]{3,2,1,0:T(8,128)} async-done(((f32[1,16,64,128]{3,2,1,0:T(8,128)}), f32[2,16,64,128]{3,2,1,0:T(8,128)}) %all-gather.16.cloned.1.call-update) | async-done | bytes 1048592 | tf_op jit(solution)/shard_map/all_gather | solution.py:26
  277.7 4.5 %add_bitcast_fusion = f32[16,64,128]{2,1,0:T(8,128)S(1)} fusion(f32[1,16,64,128]{3,2,1,0:T(8,128)} %get-tuple-element.378, f32[1,16,64,128]{3,2,1,0:T(8,128)} %get-tuple-element.332, f32[1,16,64,128]{3,2,1,0:T(8,128)} %get-tuple-element.333, f32[2,16,64,128]{3,2,1,0:T(8,128)} %all-gather.16.cloned.1.call-done, ...), kind=kLoop, calls=%fused_computation.106 | loop fusion | flops 4849664 | bytes 7917582 | tf_op jit(solution)/shard_map/mul | solution.py:157
  282.2 1.3 fusion.5
  283.7 3.4 %fusion.1 = f32[2,64,16,64]{3,1,2,0:T(8,128)} fusion(f32[2,64,16,64]{3,1,2,0:T(8,128)S(1)} %fusion.5, f32[2,16,64,64]{3,2,1,0:T(8,128)S(1)} %copy-done.6, f32[2,16,64,64]{3,1,2,0:T(8,128)S(1)} %fusion.93, f32[2,64,16,64]{3,1,2,0:T(8,128)S(1)} %copy-done.3), kind=kOutput, calls=%fused_computation.12 | convolution fusion | flops 101187584 | bytes 2621440 | tf_op jit(solution)/shard_map/nhij,nhik->nhjk/dot_general | solution.py:165
  287.2 1.6 copy.114
  288.8 1.4 reshape_reshape.7
  290.2 4.5 %all-to-all-start.1 = ((f32[2,128,8,64]{1,3,2,0:T(8,128)}), f32[2,128,8,64]{1,3,2,0:T(8,128)S(1)}, u32[]{:S(2)}, u32[]{:S(2)}) async-start(f32[2,128,8,64]{1,3,2,0:T(8,128)} %bitcast.400), calls=%async_computation.1 | async-start | bytes 1048576 | tf_op jit(solution)/shard_map/all_to_all | solution.py:69
  294.6 1.8 reduce_sum.55
  297.2 1.2 fusion.91
  299.6 10.2 %all-to-all-start.4 = ((f32[64,1,512]{2,1,0:T(1,128)}), f32[64,1,512]{2,1,0:T(1,128)S(1)}, u32[]{:S(2)}, u32[]{:S(2)}) async-start(f32[64,1,512]{2,1,0:T(1,128)} %reshape.352), calls=%async_computation.4 | async-start | bytes 262144 | tf_op jit(solution)/shard_map/all_to_all | solution.py:38
  310.4 1.4 reduce_window_sum.60
  312.0 5.4 %fusion.31 = f32[16,64,128]{2,1,0:T(8,128)} fusion(f32[2,16,64,128]{3,2,1,0:T(8,128)} %all-gather.16.cloned.1.call-done, f32[8,16,64,128]{3,2,1,0:T(8,128)} %all-gather.14.cloned.1.call-done, f32[64,64,128]{2,1,0:T(8,128)S(1)} %copy-done.2, f32[16,64]{1,0:T(8,128)S(1)} %get-tuple-element.369, f32[16,64]{1,0:T(8,128)S(1)} %get-tuple-element.371, ...), kind=kLoop, calls=%fused_computation.73 | loop fusion | flops 5636096 | bytes 7929870 | tf_op jit(solution)/shard_map/add | solution.py:101
  317.5 3.8 %all-to-all-done.4 = f32[64,1,512]{2,1,0:T(1,128)S(1)} async-done(((f32[64,1,512]{2,1,0:T(1,128)}), f32[64,1,512]{2,1,0:T(1,128)S(1)}, u32[]{:S(2)}, u32[]{:S(2)}) %all-to-all-start.4) | async-done | bytes 131104 | tf_op jit(solution)/shard_map/all_to_all | solution.py:38
  321.3 3.5 %all-to-all-start.3 = ((f32[16,64,128]{2,1,0:T(8,128)}), f32[16,64,128]{2,1,0:T(8,128)S(1)}, u32[]{:S(2)}, u32[]{:S(2)}) async-start(f32[16,64,128]{2,1,0:T(8,128)} %fusion.31), calls=%async_computation.3 | async-start | bytes 1048576 | tf_op jit(solution)/shard_map/all_to_all | solution.py:201
  325.3 0.9 reduce.4
  327.4 1.0 reshape.323
  328.5 2.4 all-to-all-done.3
  331.0 1.2 fusion.6
  332.2 1.1 copy.123
  (174 shorter events, 22.3 us)
Async XLA Ops:
  7.2 15.3 %copy-start.20 = (bf16[128,16,64]{0,2,1:T(8,128)(2,1)S(1)}, bf16[128,16,64]{0,2,1:T(8,128)(2,1)}, u32[]{:S(2)}) copy-start(bf16[128,16,64]{0,2,1:T(8,128)(2,1)} %param.11) | copy-start | bytes 786436
  7.2 62.9 %all-gather.20.cloned.1.call-start = ((), (), s32[]{:S(2)}) async-start(), calls=%async_computation.10 | async-start | bytes 2621440 | tf_op jit(solution)/shard_map/all_gather | solution.py:26
  22.4 3.8 %copy-start.8 = (bf16[128,16,128]{2,1,0:T(8,128)(2,1)S(1)}, bf16[128,16,128]{2,1,0:T(8,128)(2,1)}, u32[]{:S(2)}) copy-start(bf16[128,16,128]{2,1,0:T(8,128)(2,1)} %param.15) | copy-start | bytes 1572868
  29.9 3.2 copy-start.18
  32.2 0.8 copy-start
  33.0 72.4 %all-gather.18.cloned.1.call-start = ((), (), s32[]{:S(2)}) async-start(), calls=%async_computation.9 | async-start | bytes 2621440 | tf_op jit(solution)/shard_map/all_gather | solution.py:26
  41.0 0.8 copy-start.1
  41.9 153.7 %all-gather.10.cloned.1.call-start = ((), (), s32[]{:S(2)}) async-start(), calls=%async_computation.5 | async-start | bytes 4718592 | tf_op jit(solution)/shard_map/all_gather | solution.py:26
  52.1 56.8 %copy-start.28 = (f32[16,64]{1,0:T(8,128)}, f32[16,64]{1,0:T(8,128)S(1)}, u32[]{:S(2)}) copy-start(f32[16,64]{1,0:T(8,128)S(1)} %get-tuple-element.373) | copy-start | bytes 12292
  105.4 4.1 %copy-start.21 = (bf16[128,16,64]{0,2,1:T(8,128)(2,1)S(1)}, bf16[128,16,64]{0,2,1:T(8,128)(2,1)}, u32[]{:S(2)}) copy-start(bf16[128,16,64]{0,2,1:T(8,128)(2,1)} %param.11) | copy-start | bytes 786436
  105.4 4.1 %copy-start.23 = (bf16[128,16,64]{0,2,1:T(8,128)(2,1)S(1)}, bf16[128,16,64]{0,2,1:T(8,128)(2,1)}, u32[]{:S(2)}) copy-start(bf16[128,16,64]{0,2,1:T(8,128)(2,1)} %param.14) | copy-start | bytes 786436
  108.9 111.5 %all-gather.14.cloned.1.call-start = ((), (), s32[]{:S(2)}) async-start(), calls=%async_computation.7 | async-start | bytes 4718592 | tf_op jit(solution)/shard_map/all_gather | solution.py:26
  109.5 63.9 %copy-start.10 = (bf16[128,16,128]{2,1,0:T(8,128)(2,1)S(1)}, bf16[128,16,128]{2,1,0:T(8,128)(2,1)}, u32[]{:S(2)}) copy-start(bf16[128,16,128]{2,1,0:T(8,128)(2,1)} %param.13) | copy-start | bytes 1572868
  110.5 64.3 %all-to-all-start.2 = ((bf16[384,16,64]{0,2,1:T(8,128)(2,1)}), bf16[384,16,64]{0,2,1:T(8,128)(2,1)}, u32[]{:S(2)}, u32[]{:S(2)}) async-start(bf16[384,16,64]{0,2,1:T(8,128)(2,1)} %pad_maximum_fusion), calls=%async_computation.2 | async-start | bytes 1572864 | tf_op jit(solution)/shard_map/all_to_all | solution.py:76
  114.8 133.7 %all-gather.12.cloned.1.call-start = ((), (), s32[]{:S(2)}) async-start(), calls=%async_computation.6 | async-start | bytes 1572864 | tf_op jit(solution)/shard_map/all_gather | solution.py:26
  170.3 8.1 %copy-start.26 = (pred[64,64]{1,0:T(8,128)(4,1)}, pred[64,64]{1,0:T(8,128)(4,1)S(1)}, u32[]{:S(2)}) copy-start(pred[64,64]{1,0:T(8,128)(4,1)S(1)} %iota_compare_fusion) | copy-start | bytes 12292
  187.4 3.7 %copy-start.15 = (f32[2,64,8,128]{3,2,1,0:T(8,128)S(1)}, f32[2,64,8,128]{3,2,1,0:T(8,128)}, u32[]{:S(2)}) copy-start(f32[2,64,8,128]{3,2,1,0:T(8,128)} %reshape.327) | copy-start | bytes 1572868
  189.3 2.8 copy-start.27
  192.1 3.5 %copy-start.24 = (f32[16,64]{1,0:T(8,128)S(1)}, f32[16,64]{1,0:T(8,128)}, u32[]{:S(2)}) copy-start(f32[16,64]{1,0:T(8,128)} %bitcast_multiply_fusion.12) | copy-start | bytes 12292
  192.1 3.5 %copy-start.40 = (f32[16,64]{1,0:T(8,128)S(1)}, f32[16,64]{1,0:T(8,128)}, u32[]{:S(2)}) copy-start(f32[16,64]{1,0:T(8,128)} %get-tuple-element.360) | copy-start | bytes 12292
  192.1 3.5 %copy-start.41 = (f32[16,64]{1,0:T(8,128)S(1)}, f32[16,64]{1,0:T(8,128)}, u32[]{:S(2)}) copy-start(f32[16,64]{1,0:T(8,128)} %get-tuple-element.364) | copy-start | bytes 12292
  199.2 78.4 %all-gather.16.cloned.1.call-start = ((), (), s32[]{:S(2)}) async-start(), calls=%async_computation.8 | async-start | bytes 1572864 | tf_op jit(solution)/shard_map/all_gather | solution.py:26
  200.6 19.8 %copy-start.30 = (f32[16,64]{1,0:T(8,128)S(1)}, f32[16,64]{1,0:T(8,128)}, u32[]{:S(2)}) copy-start(f32[16,64]{1,0:T(8,128)} %get-tuple-element.352) | copy-start | bytes 12292
  200.6 19.8 %copy-start.32 = (f32[16,64]{1,0:T(8,128)S(1)}, f32[16,64]{1,0:T(8,128)}, u32[]{:S(2)}) copy-start(f32[16,64]{1,0:T(8,128)} %get-tuple-element.356) | copy-start | bytes 12292
  220.4 28.2 %copy-start.7 = (f32[64,64,128]{2,1,0:T(8,128)S(1)}, f32[64,64,128]{2,1,0:T(8,128)}, u32[]{:S(2)}) copy-start(f32[64,64,128]{2,1,0:T(8,128)} %all-gather.18.cloned.1.call-done) | copy-start | bytes 6291460
  220.4 28.2 %copy-start.25 = (f32[16,64]{1,0:T(8,128)S(1)}, f32[16,64]{1,0:T(8,128)}, u32[]{:S(2)}) copy-start(f32[16,64]{1,0:T(8,128)} %bitcast_multiply_fusion.12) | copy-start | bytes 12292
  220.4 28.2 %copy-start.43 = (f32[16,64]{1,0:T(8,128)S(1)}, f32[16,64]{1,0:T(8,128)}, u32[]{:S(2)}) copy-start(f32[16,64]{1,0:T(8,128)} %get-tuple-element.380) | copy-start | bytes 12292
  220.4 28.2 %copy-start.44 = (f32[16,64]{1,0:T(8,128)S(1)}, f32[16,64]{1,0:T(8,128)}, u32[]{:S(2)}) copy-start(f32[16,64]{1,0:T(8,128)} %get-tuple-element.381) | copy-start | bytes 12292
  220.4 28.2 %copy-start.45 = (f32[16,64]{1,0:T(8,128)S(1)}, f32[16,64]{1,0:T(8,128)}, u32[]{:S(2)}) copy-start(f32[16,64]{1,0:T(8,128)} %get-tuple-element.334) | copy-start | bytes 12292
  220.5 28.2 %copy-start.46 = (f32[16,64]{1,0:T(8,128)S(1)}, f32[16,64]{1,0:T(8,128)}, u32[]{:S(2)}) copy-start(f32[16,64]{1,0:T(8,128)} %get-tuple-element.335) | copy-start | bytes 12292
  248.6 4.5 %copy-start.9 = (bf16[128,16,128]{2,1,0:T(8,128)(2,1)S(1)}, bf16[128,16,128]{2,1,0:T(8,128)(2,1)}, u32[]{:S(2)}) copy-start(bf16[128,16,128]{2,1,0:T(8,128)(2,1)} %param.15) | copy-start | bytes 1572868
  248.6 4.5 %copy-start.12 = (f32[2,16,64,128]{3,2,1,0:T(8,128)S(1)}, f32[2,16,64,128]{3,2,1,0:T(8,128)}, u32[]{:S(2)}) copy-start(f32[2,16,64,128]{3,2,1,0:T(8,128)} %get-tuple-element.239) | copy-start | bytes 3145732
  248.6 4.5 %copy-start.39 = (f32[2,16,64]{2,1,0:T(8,128)S(1)}, f32[2,16,64]{2,1,0:T(8,128)}, u32[]{:S(2)}) copy-start(f32[2,16,64]{2,1,0:T(8,128)} %get-tuple-element.342) | copy-start | bytes 24580
  253.1 1.2 copy-start.4
  253.1 1.5 copy-start.5
  257.7 19.9 %copy-start.2 = (f32[64,64,128]{2,1,0:T(8,128)S(1)}, f32[64,64,128]{2,1,0:T(8,128)}, u32[]{:S(2)}) copy-start(f32[64,64,128]{2,1,0:T(8,128)} %all-gather.20.cloned.1.call-done) | copy-start | bytes 6291460
  257.7 19.9 %copy-start.34 = (f32[16,64]{1,0:T(8,128)S(1)}, f32[16,64]{1,0:T(8,128)}, u32[]{:S(2)}) copy-start(f32[16,64]{1,0:T(8,128)} %get-tuple-element.376) | copy-start | bytes 12292
  257.7 19.9 %copy-start.35 = (f32[16,64]{1,0:T(8,128)S(1)}, f32[16,64]{1,0:T(8,128)}, u32[]{:S(2)}) copy-start(f32[16,64]{1,0:T(8,128)} %get-tuple-element.377) | copy-start | bytes 12292
  257.7 19.9 %copy-start.36 = (f32[16,64]{1,0:T(8,128)S(1)}, f32[16,64]{1,0:T(8,128)}, u32[]{:S(2)}) copy-start(f32[16,64]{1,0:T(8,128)} %get-tuple-element.330) | copy-start | bytes 12292
  257.7 19.9 %copy-start.37 = (f32[16,64]{1,0:T(8,128)S(1)}, f32[16,64]{1,0:T(8,128)}, u32[]{:S(2)}) copy-start(f32[16,64]{1,0:T(8,128)} %get-tuple-element.331) | copy-start | bytes 12292
  262.8 27.4 %all-to-all-start = ((f32[2,128,8,64]{1,3,2,0:T(8,128)}), f32[2,128,8,64]{1,3,2,0:T(8,128)}, u32[]{:S(2)}, u32[]{:S(2)}) async-start(f32[2,128,8,64]{1,3,2,0:T(8,128)} %bitcast.399), calls=%async_computation | async-start | bytes 1048576 | tf_op jit(solution)/shard_map/all_to_all | solution.py:69
  277.6 4.6 %copy-start.11 = (bf16[128,16,128]{2,1,0:T(8,128)(2,1)S(1)}, bf16[128,16,128]{2,1,0:T(8,128)(2,1)}, u32[]{:S(2)}) copy-start(bf16[128,16,128]{2,1,0:T(8,128)(2,1)} %param.13) | copy-start | bytes 1572868
  277.6 4.5 %copy-start.14 = (f32[2,16,64,128]{3,2,1,0:T(8,128)S(1)}, f32[2,16,64,128]{3,2,1,0:T(8,128)}, u32[]{:S(2)}) copy-start(f32[2,16,64,128]{3,2,1,0:T(8,128)} %get-tuple-element.241) | copy-start | bytes 3145732
  277.6 4.5 %copy-start.38 = (f32[2,16,64]{2,1,0:T(8,128)S(1)}, f32[2,16,64]{2,1,0:T(8,128)}, u32[]{:S(2)}) copy-start(f32[2,16,64]{2,1,0:T(8,128)} %get-tuple-element.375) | copy-start | bytes 24580
  282.2 1.4 copy-start.3
  282.2 1.5 copy-start.6
  288.8 8.4 %copy-start.19 = (bf16[128,16,64]{0,2,1:T(8,128)(2,1)S(1)}, bf16[128,16,64]{0,2,1:T(8,128)(2,1)}, u32[]{:S(2)}) copy-start(bf16[128,16,64]{0,2,1:T(8,128)(2,1)} %param.12) | copy-start | bytes 786436
  290.2 7.0 %copy-start.22 = (bf16[128,16,64]{0,2,1:T(8,128)(2,1)S(1)}, bf16[128,16,64]{0,2,1:T(8,128)(2,1)}, u32[]{:S(2)}) copy-start(bf16[128,16,64]{0,2,1:T(8,128)(2,1)} %param.11) | copy-start | bytes 786436
  290.2 6.3 %all-to-all-start.1 = ((f32[2,128,8,64]{1,3,2,0:T(8,128)}), f32[2,128,8,64]{1,3,2,0:T(8,128)S(1)}, u32[]{:S(2)}, u32[]{:S(2)}) async-start(f32[2,128,8,64]{1,3,2,0:T(8,128)} %bitcast.400), calls=%async_computation.1 | async-start | bytes 1048576 | tf_op jit(solution)/shard_map/all_to_all | solution.py:69
  298.4 13.6 %copy-start.29 = (f32[16,64]{1,0:T(8,128)S(1)}, f32[16,64]{1,0:T(8,128)}, u32[]{:S(2)}) copy-start(f32[16,64]{1,0:T(8,128)} %copy-done.28) | copy-start | bytes 12292
  298.4 13.6 %copy-start.31 = (f32[16,64]{1,0:T(8,128)S(1)}, f32[16,64]{1,0:T(8,128)}, u32[]{:S(2)}) copy-start(f32[16,64]{1,0:T(8,128)} %get-tuple-element.352) | copy-start | bytes 12292
  298.4 13.6 %copy-start.33 = (f32[16,64]{1,0:T(8,128)S(1)}, f32[16,64]{1,0:T(8,128)}, u32[]{:S(2)}) copy-start(f32[16,64]{1,0:T(8,128)} %get-tuple-element.356) | copy-start | bytes 12292
  299.6 21.7 %all-to-all-start.4 = ((f32[64,1,512]{2,1,0:T(1,128)}), f32[64,1,512]{2,1,0:T(1,128)S(1)}, u32[]{:S(2)}, u32[]{:S(2)}) async-start(f32[64,1,512]{2,1,0:T(1,128)} %reshape.352), calls=%async_computation.4 | async-start | bytes 262144 | tf_op jit(solution)/shard_map/all_to_all | solution.py:38
  312.0 14.3 %copy-start.47 = (pred[64]{0:T(512)(128)(4,1)S(1)}, pred[64]{0:T(512)(128)(4,1)}, u32[]{:S(2)}) copy-start(pred[64]{0:T(512)(128)(4,1)} %iota_compare_fusion.2) | copy-start | bytes 196
  321.3 9.6 %all-to-all-start.3 = ((f32[16,64,128]{2,1,0:T(8,128)}), f32[16,64,128]{2,1,0:T(8,128)S(1)}, u32[]{:S(2)}, u32[]{:S(2)}) async-start(f32[16,64,128]{2,1,0:T(8,128)} %fusion.31), calls=%async_computation.3 | async-start | bytes 1048576 | tf_op jit(solution)/shard_map/all_to_all | solution.py:201
  326.6 4.4 %copy-start.13 = (f32[2,8,128,128]{3,2,1,0:T(8,128)S(1)}, f32[2,8,128,128]{3,2,1,0:T(8,128)}, u32[]{:S(2)}) copy-start(f32[2,8,128,128]{3,2,1,0:T(8,128)} %get-tuple-element.243) | copy-start | bytes 3145732
  326.6 4.4 %copy-start.16 = (f32[2,8,64,128]{3,2,1,0:T(8,128)S(1)}, f32[2,8,64,128]{3,2,1,0:T(8,128)}, u32[]{:S(2)}) copy-start(f32[2,8,64,128]{3,2,1,0:T(8,128)} %fusion.62) | copy-start | bytes 1572868
  326.6 4.4 %copy-start.17 = (f32[2,8,64,128]{3,1,2,0:T(8,128)S(1)}, f32[2,8,64,128]{3,1,2,0:T(8,128)}, u32[]{:S(2)}) copy-start(f32[2,8,64,128]{3,1,2,0:T(8,128)} %get-tuple-element.340) | copy-start | bytes 1572868
  326.6 4.4 %copy-start.42 = (f32[2,8,128]{2,1,0:T(8,128)S(1)}, f32[2,8,128]{2,1,0:T(8,128)}, u32[]{:S(2)}) copy-start(f32[2,8,128]{2,1,0:T(8,128)} %fusion.9) | copy-start | bytes 24580
Sparse Core Ops, SparseCore 0:
  33.1 36.9 all-gather.19
  71.9 33.4 all-gather.17
  109.0 55.7 all-gather.9
  167.1 53.2 all-gather.13
  222.1 26.4 all-gather.11
  250.2 27.3 all-gather.15
where the time goes:
time: 342 us; the launch traced here: 340 us
  waiting for transfers between devices  112 us (33%)
  other arithmetic  65.8 us (19%)
  blocking collectives  63.7 us (19%)
  local copies, waits for them, and re-layouts  35.3 us (10%)
  starting transfers between devices  27.9 us (8%)
  matrix products  20.5 us (6%)
  between operations  15.1 us (4%)
    all_gather x6, waiting for transfers between devices, prefix_by_axis(): pieces = jax.tree.map(lambda part: lax.all_gather(part, axis), total)  105 us
    all_gather x5, blocking collectives, prefix_by_axis(): pieces = jax.tree.map(lambda part: lax.all_gather(part, axis), total)  63.7 us
    add x4, other arithmetic, compose(): return (earlier[0] * later[0], later[0][..., None] * earlier[1] + later[1])  16.3 us
    another operation x1, other arithmetic, gradient_core(): cumulative = jnp.cumsum(to_blocks(log_decays, TILE_LEN), axis=2)  13.2 us
    all_to_all x1, starting transfers between devices, from_everyone(): return lax.all_to_all(copies, axis, split_axis=0, concat_axis=0, tiled=True)  10.2 us
    all_to_all x2, starting transfers between devices, summed_on_arrival(): lax.all_to_all(parts, axis, split_axis=0, concat_axis=0, tiled=True)  9.49 us
    transpose x5, local copies, waits for them, and re-layouts, to_blocks(): return tensor.astype(jnp.float32).reshape(row_count // length, length, he...  8.59 us
  transfers between devices with their start and end apart: 11, of which 7 were waited for; matrix products, arithmetic and copies ran while one was open for 25% of the time, Pallas kernels for 0%

commit v1 on v0

v1 whole, which is shorter than its diff:
```python
import functools

import jax
import jax.numpy as jnp
from jax import lax
from jax.experimental import pallas as pl
from jax.experimental.pallas import tpu as pltpu
from jax.sharding import Mesh
from jax.sharding import PartitionSpec as P

DK = 128
SA = ("sa_0", "sa_1", "sa_2")
MESH = pl.DeviceIdType.MESH
F32, BF16 = jnp.float32, jnp.bfloat16
ROWS = 128
HALF = 64


def dot(a, b, dims):
    return lax.dot_general(a, b, (dims, ((), ())), preferred_element_type=F32)


NN, NT, TN = ((1,), (0,)), ((1,), (1,)), ((0,), (0,))


def split(x):
    hi = x.astype(BF16)
    return hi, (x - hi.astype(F32)).astype(BF16)


def both(x):
    hi, lo = split(x)
    return hi, jnp.concatenate([hi, lo], axis=0)


def folded(x):
    n = x.shape[0] // 2
    return x[:n] + x[n:]


def iotas(shape):
    return lax.broadcasted_iota(jnp.int32, shape, 0), lax.broadcasted_iota(jnp.int32, shape, 1)


def kernel(
    sizes,
    q_ref, k_ref, g_ref, v_ref, o_ref,
    dq_ref, dk_ref, dg_ref, dv_ref,
    vx, ox, qx, kx, gx,
    rloc, floc, lrow, lown,
    xr, xf, xl, xe,
    zsr, zsf, zr, zf, por, pof, cr, cf,
    sir, sif, rin, fin, da, db,
    ecum, eaft, dql, dkl, kend, dvl,
    early_s, early_r, p1_s, p1_r, p2_s, p2_r, p3_s, p3_r, p4_s, p4_r, fw_s, fw_r,
):
    ny, nz, nx = sizes
    np_ = ny * nz
    rp = ROWS // np_
    y, z, x = (lax.axis_index(name) for name in SA)
    a, b = lax.axis_index("ka"), lax.axis_index("vert")
    p = y * nz + z
    na, nb = 1 - a, 1 - b
    factor = DK ** (-0.5)

    def at_x(j):
        return (y, z, j, a, b)

    def at_p(j):
        return (j // nz, lax.rem(j, nz), x, a, b)

    def rdma(src, dst, ssem, rsem, dev):
        return pltpu.make_async_remote_copy(
            src_ref=src, dst_ref=dst, send_sem=ssem, recv_sem=rsem,
            device_id=dev, device_id_type=MESH,
        )

    barrier = pltpu.get_barrier_semaphore()
    for d in range(1, nx):
        pl.semaphore_signal(barrier, inc=1, device_id=at_x(lax.rem(x + d, nx)), device_id_type=MESH)

    def greet(d, carry):
        pl.semaphore_signal(
            barrier, inc=1, device_id=at_p(lax.rem(p + d, np_)), device_id_type=MESH
        )
        return carry

    lax.fori_loop(1, np_, greet, 0)
    for dev in ((y, z, x, a, nb), (y, z, x, na, b), (y, z, x, na, nb)):
        pl.semaphore_signal(barrier, inc=1, device_id=dev, device_id_type=MESH)

    jj, ii = iotas((ROWS, 4 * ROWS))
    col = lax.rem(ii, ROWS)
    kind = ii // ROWS
    upto = (jj <= col).astype(F32)
    first = (jj < ROWS // 2).astype(F32)
    sums = jnp.where(
        kind == 0, upto - first, jnp.where(kind == 1, upto, jnp.where(kind == 2, 1.0 - upto, 1.0))
    ).astype(BF16)
    ones8 = jnp.ones((8, ROWS), BF16)
    si, sj = iotas((ROWS, ROWS))
    lower = si >= sj

    pl.semaphore_wait(barrier, nx - 1 + np_ - 1 + 3)

    own8, oth8 = b * 8, nb * 8
    early = [
        rdma(o_ref.at[pl.ds(oth8, 8)], ox, early_s.at[0], early_r.at[0], (y, z, x, a, nb)),
        rdma(v_ref.at[pl.ds(oth8, 8)], vx, early_s.at[1], early_r.at[1], (y, z, x, a, nb)),
    ]
    oth512 = pl.multiple_of(na * 512, 512)
    for n, (src, dst) in enumerate(((q_ref, qx), (k_ref, kx), (g_ref, gx))):
        early.append(
            rdma(src.at[pl.ds(oth512, 512)], dst, early_s.at[2 + n], early_r.at[2 + n],
                 (y, z, x, na, b))
        )
    for copy in early:
        copy.start()

    def rows_of(h):
        return pl.ds(pl.multiple_of(h * HALF, HALF), HALF)

    def wide(own_ref, other, h):
        return jnp.concatenate([own_ref[own8 + h], other[h]], axis=1)

    def decays(h, carry):
        sums_h = dot(g_ref[rows_of(own8 + h)], sums, NN)
        r = rows_of(h)
        dql[r] = sums_h[:, :ROWS]
        ecum[r] = jnp.exp(sums_h[:, ROWS : 2 * ROWS])
        eaft[r] = jnp.exp(sums_h[:, 2 * ROWS : 3 * ROWS])
        lown[r] = sums_h[:, 3 * ROWS :]
        return carry

    lax.fori_loop(0, 8, decays, 0)
    for i in range(nx):
        lrow[i] = dot(ones8, g_ref[pl.ds(pl.multiple_of((own8 + 2 * i) * HALF, 128), 128)], NT)

    early[0].wait_recv()

    def p1(kind, i):
        src, dst = ((rloc, xr), (floc, xf), (lrow, xl))[kind]
        return rdma(src.at[i], dst.at[x], p1_s.at[kind, i], p1_r.at[kind, x], at_x(i))

    def p1_wait(kind, j):
        dst = (xr, xf, xl)[kind]
        rdma(dst.at[j], dst.at[j], p1_s.at[kind, j], p1_r.at[kind, j], at_x(j)).wait_recv()

    for i in range(nx):
        pl.when(i != x)(p1(2, i).start)

    def states(kind, i):
        for s in range(2):
            h = 2 * i + s
            r = rows_of(h)
            if kind == 0:
                left = q_ref[rows_of(own8 + h)].astype(F32) * factor * ecum[r]
                right = wide(o_ref, ox, h)
            else:
                left = k_ref[rows_of(own8 + h)].astype(F32) * eaft[r]
                right = wide(v_ref, vx, h)
            (rloc, floc)[kind][i, s * HALF : (s + 1) * HALF] = folded(dot(both(left)[1], right, NN))
        pl.when(i != x)(p1(kind, i).start)

    for i in range(nx):
        states(0, i)
    early[1].wait_recv()
    for i in range(nx):
        states(1, i)

    def local(h, carry):
        r = rows_of(h)
        rel = dql[r]
        grow, shrink = jnp.exp(rel), jnp.exp(-rel)
        scores = jnp.where(lower, dot(wide(o_ref, ox, h), wide(v_ref, vx, h), NT), 0.0)
        s_hi, s_lo = split(scores)
        k_hi, k_two = both(k_ref[rows_of(own8 + h)].astype(F32) * shrink)
        q_hi, q_two = both(q_ref[rows_of(own8 + h)].astype(F32) * factor * grow)
        dql[r] = (folded(dot(k_two, s_hi, NT)) + dot(k_hi, s_lo, NT)) * grow * factor
        dkl[r] = (folded(dot(q_two, s_hi, NN)) + dot(q_hi, s_lo, NN)) * shrink
        return carry

    lax.fori_loop(0, 8, local, 0)

    def widen(log_row):
        return jnp.exp(jnp.broadcast_to(log_row[0:1], (ROWS, ROWS)).T)

    def scaled(state, decay):
        return state * jnp.concatenate([decay, decay], axis=1)

    for j in range(nx):
        @pl.when(j == x)
        def _own():
            xr[j] = rloc[j]
            xf[j] = floc[j]
            xl[j] = lrow[j]

        @pl.when(j != x)
        def _wait():
            p1_wait(2, j)
            p1_wait(0, j)

        xe[j] = widen(xl[j])

    row_log = xl[0]
    for j in range(1, nx):
        row_log = row_log + xl[j]
    row_log = jnp.broadcast_to(row_log[0:1], (ROWS, ROWS)).T
    total = xr[nx - 1]
    for j in reversed(range(nx - 1)):
        total = scaled(total, xe[j]) + xr[j]
    zsr[:, :, : 2 * ROWS] = total.reshape(np_, rp, 2 * ROWS)
    zsr[:, :, 2 * ROWS :] = row_log.reshape(np_, rp, ROWS)

    def p2(kind, j):
        src, dst = ((zsr, zr), (zsf, zf))[kind]
        return rdma(src.at[j], dst.at[p], p2_s.at[kind, j], p2_r.at[kind, p], at_p(j))

    def p3(kind, j):
        src, dst = ((por, cr), (pof, cf))[kind]
        return rdma(src.at[j], dst.at[p], p3_s.at[kind, j], p3_r.at[kind, p], at_p(j))

    def to_all(make):
        def body(d, carry):
            make(lax.rem(p + d, np_)).start()
            return carry

        lax.fori_loop(1, np_, body, 0)

    def from_all(dst, ssem, rsem):
        def body(d, carry):
            j = lax.rem(p + d, np_)
            rdma(dst.at[j], dst.at[j], ssem.at[j], rsem.at[j], at_p(j)).wait_recv()
            return carry

        lax.fori_loop(1, np_, body, 0)

    to_all(functools.partial(p2, 0))
    zr[p] = zsr[p]

    for j in range(nx):
        @pl.when(j != x)
        def _wait():
            p1_wait(1, j)

    total = xf[0]
    for j in range(1, nx):
        total = scaled(total, xe[j]) + xf[j]
    zsf[...] = total.reshape(np_, rp, 2 * ROWS)
    to_all(functools.partial(p2, 1))
    zf[p] = zsf[p]

    for copy in early[2:]:
        copy.wait_recv()
    first_h = a * 8

    def value_local(h, carry):
        mine, theirs = rows_of(first_h + h), rows_of(h)
        g = jnp.concatenate([g_ref[mine], gx[theirs]], axis=0)
        sums_h = dot(g, sums[:, : 3 * ROWS], NN)
        rel = sums_h[:, :ROWS]
        qs = jnp.concatenate([q_ref[mine], qx[theirs]], axis=0).astype(F32) * factor
        ks = jnp.concatenate([k_ref[mine], kx[theirs]], axis=0).astype(F32)
        q_hi, q_lo = split(qs * jnp.exp(rel))
        k_hi, k_lo = split(ks * jnp.exp(-rel))
        kend[h] = ks * jnp.exp(sums_h[:, 2 * ROWS :])
        weights = dot(k_hi, q_hi, TN) + dot(k_hi, q_lo, TN) + dot(k_lo, q_hi, TN)
        weights = jnp.where(si <= sj, weights, 0.0)
        dvl[h] = folded(dot(both(weights)[1], o_ref[first_h + h], NN))
        return carry

    lax.fori_loop(0, 8, value_local, 0)

    from_all(zr, p2_s.at[0], p2_r.at[0])
    por[np_ - 1] = jnp.zeros((rp, 2 * ROWS), F32)
    run = zr[np_ - 1][:, : 2 * ROWS]
    for j in reversed(range(np_ - 1)):
        por[j] = run
        if j > 0:
            run = scaled(run, jnp.exp(zr[j][:, 2 * ROWS :])) + zr[j][:, : 2 * ROWS]
    to_all(functools.partial(p3, 0))
    cr[p] = por[p]

    from_all(zf, p2_s.at[1], p2_r.at[1])
    pof[0] = jnp.zeros((rp, 2 * ROWS), F32)
    run = zf[0]
    for j in range(1, np_):
        pof[j] = run
        if j < np_ - 1:
            run = scaled(run, jnp.exp(zr[j][:, 2 * ROWS :])) + zf[j]
    to_all(functools.partial(p3, 1))
    cf[p] = pof[p]

    def p4(kind, j):
        src, dst = ((sir, rin), (sif, fin))[kind]
        return rdma(src.at[j], dst.at[x], p4_s.at[kind, j], p4_r.at[kind, x], at_x(j))

    from_all(cr, p3_s.at[0], p3_r.at[0])
    run = cr[...].reshape(ROWS, 2 * ROWS)
    for j in reversed(range(nx)):
        sir[j] = run
        pl.when(j != x)(p4(0, j).start)
        if j > 0:
            run = scaled(run, xe[j]) + xr[j]
    rin[x] = sir[x]

    from_all(cf, p3_s.at[1], p3_r.at[1])
    run = cf[...].reshape(ROWS, 2 * ROWS)
    for j in range(nx):
        sif[j] = run
        pl.when(j != x)(p4(1, j).start)
        if j < nx - 1:
            run = scaled(run, xe[j]) + xf[j]
    fin[x] = sif[x]

    def lanes(half):
        return pl.ds(pl.multiple_of(half * ROWS, ROWS), ROWS)

    def forward(i, core):
        half = lax.rem(core + b, 2)
        return rdma(rin.at[i, :, lanes(half)], db.at[i], fw_s.at[core, i], fw_r.at[0, i],
                    (y, z, x, na, core))

    def across(i):
        return rdma(rin.at[i, :, lanes(1)], da.at[i], fw_s.at[0, i], fw_r.at[1, i],
                    (y, z, x, a, nb))

    def send_on(i):
        @pl.when(a != b)
        def _chip():
            forward(i, 0).start()
            forward(i, 1).start()

        @pl.when(a == b)
        def _core():
            across(i).start()

    for d in range(nx):
        j = lax.rem(x + d, nx)
        if d > 0:
            rdma(rin.at[j], rin.at[j], p4_s.at[0, j], p4_r.at[0, j], at_x(j)).wait_recv()
        send_on(j)

    def key_carried(h, carry):
        r = rows_of(h)
        state = rin[h // 2, rows_of(lax.rem(h, 2))]
        dkl[r] += folded(dot(both(state)[1], wide(v_ref, vx, h), NT)) * eaft[r]
        return carry

    lax.fori_loop(0, 8, key_carried, 0)

    for d in range(1, nx):
        j = lax.rem(x + d, nx)
        rdma(fin.at[j], fin.at[j], p4_s.at[1, j], p4_r.at[1, j], at_x(j)).wait_recv()

    later = (si >= sj).astype(BF16)

    def finish(h, carry):
        r = rows_of(h)
        i, sub = h // 2, rows_of(lax.rem(h, 2))
        state = fin[i, sub]
        dq = dql[r] + folded(dot(both(state)[1], wide(o_ref, ox, h), NT)) * ecum[r] * factor
        dk = dkl[r]
        dq_ref[r] = dq
        dk_ref[r] = dk
        final = scaled(state, jnp.exp(lown[r])) + floc[i, sub]
        beyond = jnp.sum(final * rin[i, sub], axis=1, keepdims=True)
        mine = rows_of(own8 + h)
        pos = q_ref[mine].astype(F32) * dq - k_ref[mine].astype(F32) * dk
        hi, mid = split(pos)
        low = (pos - hi.astype(F32) - mid.astype(F32)).astype(BF16)
        inside = dot(jnp.concatenate([hi, mid, low], axis=0), later, NN)
        dg_ref[r] = (inside[:HALF] + inside[HALF : 2 * HALF]) + inside[2 * HALF :] + beyond
        return carry

    lax.fori_loop(0, 8, finish, 0)

    for i in range(nx):
        rdma(db.at[i], db.at[i], fw_s.at[0, i], fw_r.at[0, i], (y, z, x, na, b)).wait_recv()

        @pl.when(a != b)
        def _take():
            rdma(da.at[i], da.at[i], fw_s.at[0, i], fw_r.at[1, i], (y, z, x, a, nb)).wait_recv()

        @pl.when(a == b)
        def _copy():
            da[i] = rin[i, :, :ROWS]

    def value_finish(h, carry):
        i, sub = h // 2, rows_of(lax.rem(h, 2))
        s_hi, s_lo = split(jnp.concatenate([da[i, sub], db[i, sub]], axis=0))
        k_hi, k_lo = split(kend[h])
        dv_ref[h] = dvl[h] + dot(k_hi, s_hi, TN) + dot(k_hi, s_lo, TN) + dot(k_lo, s_hi, TN)
        return carry

    lax.fori_loop(0, 8, value_finish, 0)

    for copy in early:
        copy.wait_send()
    for i in range(nx):
        @pl.when(i != x)
        def _sent():
            for kind in range(3):
                p1(kind, i).wait_send()
            for kind in range(2):
                p4(kind, i).wait_send()

        @pl.when(a != b)
        def _sent_chip():
            forward(i, 0).wait_send()
            forward(i, 1).wait_send()

        @pl.when(a == b)
        def _sent_core():
            across(i).wait_send()

    def sent(d, carry):
        j = lax.rem(p + d, np_)
        for kind in range(2):
            p2(kind, j).wait_send()
            p3(kind, j).wait_send()
        return carry

    lax.fori_loop(1, np_, sent, 0)


def shards(sizes, queries, key_rows, values, log_decays, output_grad):
    ny, nz, nx = sizes
    np_ = ny * nz
    rp = ROWS // np_
    qt, kt, gt = (t.transpose(1, 2, 0).reshape(-1, ROWS) for t in (queries, key_rows, log_decays))
    vh, oh = (t.transpose(1, 0, 2) for t in (values, output_grad))
    vmem = pl.BlockSpec(memory_space=pltpu.VMEM)
    dma = pltpu.SemaphoreType.DMA

    def f32(*shape):
        return pltpu.VMEM(shape, F32)

    def bf16(*shape):
        return pltpu.VMEM(shape, BF16)

    sq, state = (ROWS, ROWS), (ROWS, 2 * ROWS)
    dq, dk, dg, dv = pl.pallas_call(
        functools.partial(kernel, sizes),
        out_shape=[jax.ShapeDtypeStruct((512, ROWS), F32)] * 3
        + [jax.ShapeDtypeStruct((8, ROWS, ROWS), F32)],
        in_specs=[vmem] * 5,
        out_specs=[vmem] * 4,
        scratch_shapes=[bf16(8, *sq)] * 2 + [bf16(512, ROWS)] * 3
        + [f32(nx, *state)] * 2 + [f32(nx, 8, ROWS), f32(512, ROWS)]
        + [f32(nx, *state)] * 2 + [f32(nx, 8, ROWS), f32(nx, *sq)]
        + [f32(np_, rp, 3 * ROWS), f32(np_, rp, 2 * ROWS)] * 2
        + [f32(np_, rp, 2 * ROWS)] * 4
        + [f32(nx, *state)] * 4 + [f32(nx, *sq)] * 2
        + [f32(512, ROWS)] * 4 + [f32(8, *sq)] * 2
        + [dma((5,))] * 2 + [dma((3, nx))] * 2 + [dma((2, np_))] * 4
        + [dma((2, nx))] * 4,
        compiler_params=pltpu.CompilerParams(collective_id=0, has_side_effects=True),
    )(qt, kt, gt, vh, oh)
    dq, dk, dg = (t.reshape(8, HALF, ROWS).transpose(2, 0, 1) for t in (dq, dk, dg))
    return dq, dk, dv.transpose(1, 0, 2), dg


def solution(mesh):
    ka, vert = mesh.shape["ka"], mesh.shape["vert"]
    sizes = (2, 8, 4)
    if mesh.shape["sa"] != 64:
        sizes = (mesh.shape["sa"] // 4, 1, 4)
    finer = Mesh(mesh.devices.reshape(*sizes, ka, vert), (*SA, "ka", "vert"))
    return jax.shard_map(
        functools.partial(shards, sizes),
        mesh=finer,
        in_specs=(P(SA, None, "ka"),) * 2 + (P(SA, None, "vert"), P(SA, None, "ka"), P(SA, None, "vert")),
        out_specs=(P(SA, "vert", "ka"), P(SA, "vert", "ka"), P(SA, "ka", "vert"), P(SA, "vert", "ka")),
        check_vma=False,
    )
```

time: 342 us -> 66.7 us (0.20)
  waiting for transfers between devices: 112 us -> 0 us
  other arithmetic: 65.8 us -> 0 us
  blocking collectives: 63.7 us -> 0 us
  Pallas kernels: 0 us -> 58.2 us
  starting transfers between devices: 27.9 us -> 0 us
  local copies, waits for them, and re-layouts: 35.3 us -> 7.42 us
  matrix products: 20.5 us -> 0 us
  between operations: 15.1 us -> 0.65 us
    all_gather x6 -> x0, waiting for transfers between devices: 105 us -> none  [prefix_by_axis(): pieces = jax.tree.map(lambda part: lax.all_gather(part, axis), total)]
    all_gather x5 -> x0, blocking collectives: 63.7 us -> none  [prefix_by_axis(): pieces = jax.tree.map(lambda part: lax.all_gather(part, axis), total)]
    pallas_call x0 -> x1, Pallas kernels: none -> 58.2 us  [shards(): pl.pallas_call(functools.partial(kernel, sizes), out_shape=[jax.ShapeDtyp...]
    all_to_all x5 -> x0, starting transfers between devices: 27.4 us -> none  [the longest x1 10.2 us: from_everyone(): return lax.all_to_all(copies, axis, split_axis=0, concat_axis=0, tiled=True)]
    dot_general x12 -> x0, matrix products: 20.5 us -> none  [the longest x2 3.5 us: backward_states(): jnp.einsum('nhik,nhiv->nhkv', amplified_query, cotangent, precision=large...]
    add x16 -> x0, other arithmetic: 18.1 us -> none  [the longest x4 16.3 us: compose(): return (earlier[0] * later[0], later[0][..., None] * earlier[1] + later[1])]
    another operation x5 -> x0, other arithmetic: 16.9 us -> none  [the longest x1 13.2 us: gradient_core(): cumulative = jnp.cumsum(to_blocks(log_decays, TILE_LEN), axis=2)]
    mul x15 -> x0, other arithmetic: 16.6 us -> none  [the longest x1 4.51 us: gradient_core(): ends = ends + jnp.exp(after)[..., None] * outgoing[None]]
  transfers between devices with their start and end apart: 11 -> 0, of which waited for: 7 -> 0; matrix products, arithmetic and copies ran while one was open for 25% -> 0% of each run, Pallas kernels for 0% -> 0%
where the time goes in v1:
time: 66.7 us; the launch traced here: 66.3 us
  Pallas kernels  58.2 us (87%)
  local copies, waits for them, and re-layouts  7.42 us (11%)
    pallas_call x1, Pallas kernels, shards(): pl.pallas_call(functools.partial(kernel, sizes), out_shape=[jax.ShapeDtyp...  58.2 us
    unnamed x10, local copies, waits for them, and re-layouts  4.98 us
    transpose x1, local copies, waits for them, and re-layouts, shards(): vh, oh = (t.transpose(1, 0, 2) for t in (values, output_grad))  2.44 us

profile of v1, /device:TPU:1, one launch (start us, length us, event | category | flops | bytes accessed | tf_op | source)
XLA Modules:
  0.0 66.3 jit_solution(13437891918743410329)
XLA Ops:
  0.6 2.4 %copy_bitcast_fusion = (bf16[16,128,128]{2,1,0:T(8,128)(2,1)}, bf16[16,128,128]{2,1,0:T(8,128)(2,1)}) fusion(bf16[128,16,128]{2,1,0:T(8,128)(2,1)} %param.9, bf16[128,16,128]{2,1,0:T(8,128)(2,1)} %param.7), kind=kLoop, calls=%fused_computation | loop fusion | bytes 2097152 | tf_op jit(solution)/shard_map/transpose | solution.py:432
  3.1 58.2 %shard_map.84 = (f32[512,128]{1,0:T(8,128)}, f32[512,128]{1,0:T(8,128)}, f32[512,128]{1,0:T(8,128)}, f32[8,128,128]{2,1,0:T(8,128)}) custom-call(bf16[1024,128]{1,0:T(8,128)(2,1)} %bitcast.24, bf16[1024,128]{1,0:T(8,128)(2,1)} %bitcast.25, bf16[1024,128]{1,0:T(8,128)(2,1)} %bitcast.26, bf16[16,128,128]{2,1,0:T(8,128)(2,1)} %get-tuple-element.17.v_ref, ...), custom_call_target="tpu_custom_call" | custom-call | tf_op jit(solution)/shard_map/pallas_call | solution.py:443
  61.3 0.0 copy-start.2
  61.3 2.2 %copy.11 = f32[128,8,128]{2,1,0:T(8,128)} copy(f32[128,8,128]{2,0,1:T(8,128)} %bitcast.23) | data formatting | bytes 1048576
  63.5 0.0 copy-done.2
  63.5 0.0 copy-start.1
  63.5 0.7 %copy.17 = f32[128,8,64]{0,2,1:T(8,128)} copy(f32[128,8,64]{0,2,1:T(8,128)S(1)} %bitcast.29) | data formatting | bytes 524288
  64.2 0.3 copy-done.1
  64.5 0.0 copy-start
  64.5 0.7 %copy.18 = f32[128,8,64]{0,2,1:T(8,128)} copy(f32[128,8,64]{0,2,1:T(8,128)S(1)} %bitcast.28) | data formatting | bytes 524288
  65.2 0.3 copy-done
  65.6 0.7 %copy.19 = f32[128,8,64]{0,2,1:T(8,128)} copy(f32[128,8,64]{0,2,1:T(8,128)S(1)} %bitcast.27) | data formatting | bytes 524288
Async XLA Ops:
  61.3 2.2 %copy-start.2 = (f32[512,128]{1,0:T(8,128)S(1)}, f32[512,128]{1,0:T(8,128)}, u32[]{:S(2)}) copy-start(f32[512,128]{1,0:T(8,128)} %get-tuple-element.8) | copy-start | bytes 786436
  63.5 1.0 %copy-start.1 = (f32[512,128]{1,0:T(8,128)S(1)}, f32[512,128]{1,0:T(8,128)}, u32[]{:S(2)}) copy-start(f32[512,128]{1,0:T(8,128)} %get-tuple-element.9) | copy-start | bytes 786436
  64.5 1.0 %copy-start = (f32[512,128]{1,0:T(8,128)S(1)}, f32[512,128]{1,0:T(8,128)}, u32[]{:S(2)}) copy-start(f32[512,128]{1,0:T(8,128)} %get-tuple-element.11) | copy-start | bytes 786436
